TPU v7x, 32 devices: a whole 2x2x4 slice. The times are simulated.
32 devices in a mesh: group: 4 (over y, x), shard: 8 (over z, core).
Axes of the slice: x: 2, y: 2, z: 4, core: 2. Of those that a mesh axis runs over, the one named last changes fastest.
Arguments:
- embeddings: bfloat16 [128, 256, 768], P(('group', 'shard')), may hold values from -6 to 6
- assignments: int32 [128, 2, 256], P(('group', 'shard')), may hold values from 0 to 4095, as said below
- block_group: int32 [128], P(('group', 'shard')), may hold values from 0 to 3, as said below
- centroids: float32 [4, 4096, 768], P('group'), may hold values from -6 to 6
Outputs:
- subcentroids: float32 [4, 4096, 768], P('group', 'shard')
- inertia: float32 [4, 4096], P('group', 'shard')
Inputs may be any that keep to these rules, and one draw needn't show every extreme that they name: `block_group`: of the 4 blocks of one device at most 2 name the same group; in every draw, for some group and some shard index, every device of that shard index has exactly 2 blocks naming that group. `assignments`: labels k with the same k // 512 form one range. In each block and iteration at most 64 rows have labels in one range; in every draw there is an iteration in which every block has exactly 64 rows in one common range.
All inputs are finite; a program needn't handle non-finite values.
Results may differ from a plain program's by a relative error of at most 0.0003.
Values may be sent and summed in bfloat16 or wider, within the bound.
A program may use at most 128 MiB of HBM per device.

v0:
```python
import jax
import jax.numpy as jnp
from jax import lax
from jax.sharding import PartitionSpec as P

K = 4096
ITERS = 2
CAP = 2


PRIOR = 8.0


def pack_blocks(embeddings, assignments, block_group, groups, slots_per):
    matches = (block_group[None, :] == lax.broadcasted_iota(jnp.int32, (groups, 1), 0)).astype(
        jnp.int32
    )
    ranking = jnp.cumsum(matches, axis=1) - 1
    slot_ids = lax.broadcasted_iota(jnp.int32, (1, slots_per, 1), 1)
    selection = matches[:, None, :] * (ranking[:, None, :] == slot_ids).astype(jnp.int32)
    filled = jnp.sum(selection, axis=2)
    sent_rows = jnp.einsum(
        "gcb,brd->gcrd",
        selection.astype(jnp.bfloat16),
        embeddings,
        preferred_element_type=jnp.float32,
    ).astype(jnp.bfloat16)
    sent_labels = (
        jnp.einsum("gcb,btr->gctr", selection, assignments) + (filled - 1)[:, :, None, None]
    )
    return (sent_rows, sent_labels)


def tally(piece_rows, piece_labels, totals, extra_kind):
    centers = totals[0].shape[0]
    onehot = piece_labels[:, None] == lax.broadcasted_iota(jnp.int32, (1, centers), 1)
    weights = onehot.astype(jnp.float32)
    center_sums = totals[0] + lax.dot_general(
        onehot.astype(jnp.bfloat16),
        piece_rows,
        (((0,), (0,)), ((), ())),
        preferred_element_type=jnp.float32,
    )
    counts = totals[1] + jnp.sum(weights, axis=0)
    if extra_kind == "none":
        return (center_sums, counts)
    widened = piece_rows.astype(jnp.float32)
    per_row = jnp.sum(widened * widened, axis=1)
    extra_total = totals[2] + jnp.dot(per_row, weights, precision=lax.Precision.HIGHEST)
    return (center_sums, counts, extra_total)


def body(embeddings, assignments, block_group, centroids):
    groups = lax.axis_size("group")
    sent_rows, sent_labels = pack_blocks(embeddings, assignments, block_group, groups, CAP)
    got_rows, got_labels = (
        lax.all_to_all(sent_rows, "group", split_axis=0, concat_axis=0, tiled=True),
        lax.all_to_all(sent_labels, "group", split_axis=0, concat_axis=0, tiled=True),
    )
    shards = lax.axis_size("shard")
    owned_rows = K // shards
    previous = lax.dynamic_slice_in_dim(
        centroids[0], lax.axis_index("shard") * owned_rows, owned_rows, 0
    )
    features = got_rows.shape[-1]
    block_rows = got_rows.shape[2]
    slot_count = got_rows.shape[0] * got_rows.shape[1]
    flat_rows = got_rows.reshape(slot_count * block_rows, features)
    inertia = jnp.zeros((owned_rows,), jnp.float32)
    for iteration in range(ITERS):
        is_last = iteration == ITERS - 1
        labels = got_labels[:, :, iteration, :]
        previous_full = None
        extra_kind = "none"
        if is_last:
            extra_kind = "squares"
        totals = (jnp.zeros((K, features), jnp.float32), jnp.zeros((K,), jnp.float32))
        if extra_kind != "none":
            totals = totals + (jnp.zeros((K,), jnp.float32),)
        piece_size = 2 * block_rows
        flat_labels = labels.reshape(-1)

        def add_piece(
            position,
            running,
            extra_kind=extra_kind,
            previous_full=previous_full,
            flat_labels=flat_labels,
        ):
            start = position * piece_size
            piece_rows = lax.dynamic_slice_in_dim(flat_rows, start, piece_size, 0)
            piece_labels = lax.dynamic_slice_in_dim(flat_labels, start, piece_size, 0)
            return tally(piece_rows, piece_labels, running, extra_kind)

        totals = lax.fori_loop(0, slot_count // 2, add_piece, totals)
        reduced = lax.psum_scatter(totals, "shard", scatter_dimension=0, tiled=True)
        if is_last:
            within = (
                reduced[2]
                - 2.0 * jnp.sum(previous * reduced[0], axis=1)
                + reduced[1] * jnp.sum(previous * previous, axis=1)
            )
            inertia = within / ((reduced[1] + PRIOR) * features)
        previous = (reduced[0] + PRIOR * previous) / (reduced[1] + PRIOR)[:, None]
    return (previous[None], inertia[None])


def solution(mesh):
    in_specs = (
        P(("group", "shard"), None, None),
        P(("group", "shard"), None, None),
        P(("group", "shard")),
        P("group", None, None),
    )
    out_specs = (P("group", "shard", None), P("group", "shard"))
    return jax.shard_map(body, mesh=mesh, in_specs=in_specs, out_specs=out_specs, check_vma=False)
```

profile of v0, /device:TPU:0, one launch (start us, length us, event | category | flops | bytes accessed | tf_op | source)
XLA Modules:
  0.0 387.4 jit_solution(1077661246669456399)
XLA Ops:
  9.7 5.2 %all-to-all-start = ((s32[4,2,2,256]{3,2,1,0:T(2,128)}), s32[4,2,2,256]{3,2,1,0:T(2,128)S(1)}, u32[]{:S(2)}, u32[]{:S(2)}) async-start(s32[4,2,2,256]{3,2,1,0:T(2,128)} %copy.18), calls=%async_computation | async-start | bytes 32768 | tf_op jit(solution)/shard_map/all_to_all | solution.py:58
  14.9 3.3 convolution_convert_fusion
  18.2 2.1 copy.20
  20.3 4.2 %all-to-all-start.1 = ((bf16[4,2,256,768]{3,2,1,0:T(8,128)(2,1)}), bf16[4,2,256,768]{3,2,1,0:T(8,128)(2,1)S(1)}, u32[]{:S(2)}, u32[]{:S(2)}) async-start(bf16[4,2,256,768]{3,2,1,0:T(8,128)(2,1)} %copy.20), calls=%async_computation.1 | async-start | bytes 6291456 | tf_op jit(solution)/shard_map/all_to_all | solution.py:57
  24.5 35.6 %all-to-all-done.1 = bf16[4,2,256,768]{3,2,1,0:T(8,128)(2,1)S(1)} async-done(((bf16[4,2,256,768]{3,2,1,0:T(8,128)(2,1)}), bf16[4,2,256,768]{3,2,1,0:T(8,128)(2,1)S(1)}, u32[]{:S(2)}, u32[]{:S(2)}) %all-to-all-start.1) | async-done | bytes 3145760 | tf_op jit(solution)/shard_map/all_to_all | solution.py:57
  60.0 54.9 %while.34 = (s32[]{:T(128)}, f32[4096,768]{1,0:T(8,128)}, f32[4096]{0:T(1024)S(1)}, f32[4096]{0:T(1024)S(1)}, s32[2048]{0:T(1024)S(1)}, /*index=5*/bf16[2048,768...) while((s32[]{:T(128)}, f32[4096,768]{1,0:T(8,128)}, f32[4096]{0:T(1024)S(1)}, ...), condition=%wide.region_5.6_spmd.clone, body=%wide.region_2.5_spmd.clone.sunk | while | flops 3264359936 | bytes 26884272 | solution.py:95
  60.1 6.5 %select_add_fusion.9 = f32[4096,768]{1,0:T(8,128)} fusion(f32[4096,768]{1,0:T(8,128)} %get-tuple-element.369, pred[]{:T(512)S(6)} %compare.6, s32[512]{0:T(512)S(1)} %dynamic_slice.50, bf16[2048,768]{1,0:T(8,128)(2,1)S(1)} %get-tuple-element.383, s32[]{:T(128)S(6)} %select_n.24), kind=kOutput, calls=%fused_computation.clone.1 | convolution fusion | flops 3229614080 | bytes 25954308 | tf_op jit(solution)/shard_map/while/body/eval_jaxpr/dot_general | solution.py:38
  66.9 2.8 fusion.37
  71.8 9.3 %select_add_fusion.9 = f32[4096,768]{1,0:T(8,128)} fusion(f32[4096,768]{1,0:T(8,128)} %get-tuple-element.369, pred[]{:T(512)S(6)} %compare.6, s32[512]{0:T(512)S(1)} %dynamic_slice.50, bf16[2048,768]{1,0:T(8,128)(2,1)S(1)} %get-tuple-element.383, s32[]{:T(128)S(6)} %select_n.24), kind=kOutput, calls=%fused_computation.clone.1 | convolution fusion | flops 3229614080 | bytes 25954308 | tf_op jit(solution)/shard_map/while/body/eval_jaxpr/dot_general | solution.py:38
  81.3 2.8 fusion.37
  86.2 9.3 %select_add_fusion.9 = f32[4096,768]{1,0:T(8,128)} fusion(f32[4096,768]{1,0:T(8,128)} %get-tuple-element.369, pred[]{:T(512)S(6)} %compare.6, s32[512]{0:T(512)S(1)} %dynamic_slice.50, bf16[2048,768]{1,0:T(8,128)(2,1)S(1)} %get-tuple-element.383, s32[]{:T(128)S(6)} %select_n.24), kind=kOutput, calls=%fused_computation.clone.1 | convolution fusion | flops 3229614080 | bytes 25954308 | tf_op jit(solution)/shard_map/while/body/eval_jaxpr/dot_general | solution.py:38
  95.7 2.8 fusion.37
  100.6 9.3 %select_add_fusion.9 = f32[4096,768]{1,0:T(8,128)} fusion(f32[4096,768]{1,0:T(8,128)} %get-tuple-element.369, pred[]{:T(512)S(6)} %compare.6, s32[512]{0:T(512)S(1)} %dynamic_slice.50, bf16[2048,768]{1,0:T(8,128)(2,1)S(1)} %get-tuple-element.383, s32[]{:T(128)S(6)} %select_n.24), kind=kOutput, calls=%fused_computation.clone.1 | convolution fusion | flops 3229614080 | bytes 25954308 | tf_op jit(solution)/shard_map/while/body/eval_jaxpr/dot_general | solution.py:38
  110.2 2.8 fusion.37
  113.0 2.0 convert_reduce_fusion.4
  115.3 43.4 %while.35 = (s32[]{:T(128)}, f32[4096,768]{1,0:T(8,128)}, f32[4096]{0:T(1024)S(1)}, s32[2048]{0:T(1024)S(1)}, bf16[2048,768]{1,0:T(8,128)(2,1)S(1)}, /*index=5*/s32[]{:T(128)}, s32[]{:T(128)}, s32[]{:T(128)}, s32[]{:T(128)}) while((s32[]{:T(128)}, f32[4096,768]{1,0:T(8,128)}, f32[4096]{0:T(1024)S(1)}, s32[2048]{0:T(1024)S(1)}, ...), condition=%wide.region_9.10_spmd.clone, body=%wide.region_7.9_spmd.clone.sunk | while | flops 3235909632 | bytes 26026148 | solution.py:95
  115.4 6.8 %select_add_fusion.11 = f32[4096,768]{1,0:T(8,128)} fusion(f32[4096,768]{1,0:T(8,128)} %get-tuple-element.398, pred[]{:T(512)S(6)} %compare.7, s32[512]{0:T(512)S(1)} %dynamic_slice.52, bf16[2048,768]{1,0:T(8,128)(2,1)S(1)} %get-tuple-element.410, s32[]{:T(128)S(6)} %select_n.25), kind=kOutput, calls=%fused_computation.12.clone.1 | convolution fusion | flops 3229614080 | bytes 25954308 | tf_op jit(solution)/shard_map/while/body/eval_jaxpr/dot_general | solution.py:38
  124.3 9.3 %select_add_fusion.11 = f32[4096,768]{1,0:T(8,128)} fusion(f32[4096,768]{1,0:T(8,128)} %get-tuple-element.398, pred[]{:T(512)S(6)} %compare.7, s32[512]{0:T(512)S(1)} %dynamic_slice.52, bf16[2048,768]{1,0:T(8,128)(2,1)S(1)} %get-tuple-element.410, s32[]{:T(128)S(6)} %select_n.25), kind=kOutput, calls=%fused_computation.12.clone.1 | convolution fusion | flops 3229614080 | bytes 25954308 | tf_op jit(solution)/shard_map/while/body/eval_jaxpr/dot_general | solution.py:38
  135.7 9.4 %select_add_fusion.11 = f32[4096,768]{1,0:T(8,128)} fusion(f32[4096,768]{1,0:T(8,128)} %get-tuple-element.398, pred[]{:T(512)S(6)} %compare.7, s32[512]{0:T(512)S(1)} %dynamic_slice.52, bf16[2048,768]{1,0:T(8,128)(2,1)S(1)} %get-tuple-element.410, s32[]{:T(128)S(6)} %select_n.25), kind=kOutput, calls=%fused_computation.12.clone.1 | convolution fusion | flops 3229614080 | bytes 25954308 | tf_op jit(solution)/shard_map/while/body/eval_jaxpr/dot_general | solution.py:38
  147.2 9.4 %select_add_fusion.11 = f32[4096,768]{1,0:T(8,128)} fusion(f32[4096,768]{1,0:T(8,128)} %get-tuple-element.398, pred[]{:T(512)S(6)} %compare.7, s32[512]{0:T(512)S(1)} %dynamic_slice.52, bf16[2048,768]{1,0:T(8,128)(2,1)S(1)} %get-tuple-element.410, s32[]{:T(128)S(6)} %select_n.25), kind=kOutput, calls=%fused_computation.12.clone.1 | convolution fusion | flops 3229614080 | bytes 25954308 | tf_op jit(solution)/shard_map/while/body/eval_jaxpr/dot_general | solution.py:38
  160.5 30.8 %all-reduce.3 = (f32[4096]{0:T(1024)S(1)}, f32[4096]{0:T(1024)S(1)}, f32[4096]{0:T(1024)S(1)}) all-reduce(f32[4096]{0:T(1024)S(1)} %get-tuple-element.210, f32[4096]{0:T(1024)S(1)} %get-tuple-element.211, f32[4096]{0:T(1024)S(1)} %get-tuple-element.212), channel_id=4, replica_groups=mesh['group'=4,'shard'=8] {'shard'}, use_global_device_ids=true, to_apply=%region_11.12.clone | all-reduce | flops 12288 | bytes 98304
  191.4 54.4 %reduce-scatter.3.cloned.1.call-done = f32[512,768]{1,0:T(8,128)} async-done(((f32[4096,768]{1,0:T(8,128)}), f32[512,768]{1,0:T(8,128)}) %reduce-scatter.3.cloned.1.call-update) | async-done | bytes 1572880 | tf_op jit(solution)/shard_map/reduce_scatter | solution.py:96
  245.8 129.9 %reduce-scatter.5.cloned.1.call-done = f32[512,768]{1,0:T(8,128)} async-done(((f32[4096,768]{1,0:T(8,128)}), f32[512,768]{1,0:T(8,128)}) %reduce-scatter.5.cloned.1.call-update) | async-done | bytes 1572880 | tf_op jit(solution)/shard_map/reduce_scatter | solution.py:96
  375.7 2.8 multiply_reduce_fusion.2
  (53 shorter events, 21.7 us)
Async XLA Ops:
  9.7 10.6 %all-to-all-start = ((s32[4,2,2,256]{3,2,1,0:T(2,128)}), s32[4,2,2,256]{3,2,1,0:T(2,128)S(1)}, u32[]{:S(2)}, u32[]{:S(2)}) async-start(s32[4,2,2,256]{3,2,1,0:T(2,128)} %copy.18), calls=%async_computation | async-start | bytes 32768 | tf_op jit(solution)/shard_map/all_to_all | solution.py:58
  20.3 39.8 %all-to-all-start.1 = ((bf16[4,2,256,768]{3,2,1,0:T(8,128)(2,1)}), bf16[4,2,256,768]{3,2,1,0:T(8,128)(2,1)S(1)}, u32[]{:S(2)}, u32[]{:S(2)}) async-start(bf16[4,2,256,768]{3,2,1,0:T(8,128)(2,1)} %copy.20), calls=%async_computation.1 | async-start | bytes 6291456 | tf_op jit(solution)/shard_map/all_to_all | solution.py:57
  24.4 221.4 %reduce-scatter.3.cloned.1.call-start = ((), (), s32[]{:S(2)}) async-start(), calls=%async_computation.4 | async-start | bytes 14155776 | tf_op jit(solution)/shard_map/reduce_scatter | solution.py:96
  115.0 260.7 %reduce-scatter.5.cloned.1.call-start = ((), (), s32[]{:S(2)}) async-start(), calls=%async_computation.5 | async-start | bytes 14155776 | tf_op jit(solution)/shard_map/reduce_scatter | solution.py:96
  158.6 0.7 copy-start.1
  245.8 133.4 %copy-start = (f32[512,768]{1,0:T(8,128)S(1)}, f32[512,768]{1,0:T(8,128)}, u32[]{:S(2)}) copy-start(f32[512,768]{1,0:T(8,128)} %reduce-scatter.3.cloned.1.call-done) | copy-start | bytes 4718596
Sparse Core Ops, SparseCore 0:
  115.1 130.6 reduce-scatter.2
  248.1 127.5 reduce-scatter.4
where the time goes:
time: 388 us; the launch traced here: 387 us
  waiting for transfers between devices  220 us (57%)
  matrix products  84.7 us (22%)
  blocking collectives  30.8 us (8%)
  other arithmetic  22.9 us (6%)
  between operations  14.8 us (4%)
  starting transfers between devices  9.61 us (2%)
  local copies, waits for them, and re-layouts  4.53 us (1%)
    reduce_scatter x2, waiting for transfers between devices, body(): reduced = lax.psum_scatter(totals, 'shard', scatter_dimension=0, tiled=True)  184 us
    dot_general x8, matrix products, tally(): lax.dot_general(onehot.astype(jnp.bfloat16), piece_rows, (((0,), (0,)), (...  69.4 us
    all_to_all x1, waiting for transfers between devices, body(): lax.all_to_all(sent_rows, 'group', split_axis=0, concat_axis=0, tiled=True)  35.6 us
    unnamed x1, blocking collectives  30.8 us
    reduce_sum x8, other arithmetic, tally(): counts = totals[1] + jnp.sum(weights, axis=0)  16 us
    dot_general x4, matrix products, tally(): jnp.dot(per_row, weights, precision=lax.Precision.HIGHEST)  11.1 us
  transfers between devices with their start and end apart: 4, of which 3 were waited for; matrix products, arithmetic and copies ran while one was open for 13% of the time, Pallas kernels for 0%

commit v1 on v0

v1 whole, which is shorter than its diff:
```python
import functools

import jax
import jax.numpy as jnp
from jax import lax
from jax.experimental import pallas as pl
from jax.experimental.pallas import tpu as pltpu
from jax.sharding import PartitionSpec as P

PRIOR = 8.0
META = 8
CHUNKS = 3
MESH = pl.DeviceIdType.MESH


def exchange_kernel(n_gather, n_swap, width, column, *refs):
    n_in = n_gather + n_swap
    gathers, swaps = refs[:n_gather], refs[n_gather:n_in]
    outs = refs[n_in : 2 * n_in]
    gather_outs, swap_outs = outs[:n_gather], outs[n_gather:]
    scratch = refs[2 * n_in :]
    stages = scratch[:n_gather]
    scratch = scratch[n_gather:]

    groups, shards = lax.axis_size("group"), lax.axis_size("shard")
    chips = shards // 2
    mine, place = lax.axis_index("group"), lax.axis_index("shard")
    chip, core = place // 2, place % 2
    partner = (mine, chip * 2 + 1 - core)
    right = (mine, lax.rem(chip + 1, chips) * 2 + core)
    left = (mine, lax.rem(chip + chips - 1, chips) * 2 + core)

    def peer(step):
        return lax.rem(mine + step, groups)

    barrier = pltpu.get_barrier_semaphore()
    greeted = 0
    if n_gather:
        for device in (left, right, partner):
            pl.semaphore_signal(barrier, inc=1, device_id=device, device_id_type=MESH)
        greeted += 3
    if n_swap:
        for step in range(1, groups):
            pl.semaphore_signal(
                barrier, inc=1, device_id=(peer(step), place), device_id_type=MESH
            )
        greeted += groups - 1

    loads = []
    if n_gather:
        load_sem = scratch[0]
        for i in range(n_gather):
            source = gathers[i]
            if i == 0:
                source = source.at[:, :, pl.ds(column, width)]
            load = pltpu.make_async_copy(source, stages[i], load_sem.at[i])
            load.start()
            loads.append(load)
    pl.semaphore_wait(barrier, greeted)

    swap_copies = []
    if n_swap:
        swap_send, swap_recv = scratch[-2:]
        for step in range(1, groups):
            for i in range(n_swap):
                copy = pltpu.make_async_remote_copy(
                    src_ref=swaps[i].at[peer(step)],
                    dst_ref=swap_outs[i].at[step - 1],
                    send_sem=swap_send.at[i, step - 1],
                    recv_sem=swap_recv.at[i, step - 1],
                    device_id=(peer(step), place),
                    device_id_type=MESH,
                )
                copy.start()
                swap_copies.append(copy)

    if n_gather:
        store_sem, send_r, recv_r, send_l, recv_l, send_p, recv_p = scratch[1:8]
        stores = []

        def hop(i, source, origin, step, to, sends, recvs):
            return pltpu.make_async_remote_copy(
                src_ref=source,
                dst_ref=gather_outs[i].at[origin * 2 + core],
                send_sem=sends.at[i, step],
                recv_sem=recvs.at[i, step],
                device_id=to,
                device_id_type=MESH,
            )

        for i in range(n_gather):
            loads[i].wait()
            store = pltpu.make_async_copy(
                stages[i], gather_outs[i].at[place], store_sem.at[i]
            )

            @pl.when(chip < chips - 1)
            def _():
                hop(i, stages[i], chip, 0, right, send_r, recv_r).start()

            @pl.when(chip > 0)
            def _():
                hop(i, stages[i], chip, 0, left, send_l, recv_l).start()

            hop(i, stages[i], chip, chip, partner, send_p, recv_p).start()
            store.start()
            stores.append(store)

        for step in range(chips - 1):
            for i in range(n_gather):
                from_left = chip - 1 - step

                @pl.when(from_left >= 0)
                def _():
                    block = gather_outs[i].at[from_left * 2 + core]
                    hop(i, block, from_left, step, right, send_r, recv_r).wait_recv()

                    if step < chips - 2:

                        @pl.when(chip < chips - 1)
                        def _():
                            hop(i, block, from_left, step + 1, right, send_r, recv_r).start()

                    hop(i, block, from_left, from_left, partner, send_p, recv_p).start()

                from_right = chip + 1 + step

                @pl.when(from_right <= chips - 1)
                def _():
                    block = gather_outs[i].at[from_right * 2 + core]
                    hop(i, block, from_right, step, left, send_l, recv_l).wait_recv()

                    if step < chips - 2:

                        @pl.when(chip > 0)
                        def _():
                            hop(i, block, from_right, step + 1, left, send_l, recv_l).start()

                    hop(i, block, from_right, from_right, partner, send_p, recv_p).start()

        for i in range(n_gather):
            stores[i].wait()
            for step in range(chips - 1):

                @pl.when((chip - step >= 0) & (chip < chips - 1))
                def _():
                    hop(i, stages[i], chip, step, right, send_r, recv_r).wait_send()

                @pl.when((chip + step <= chips - 1) & (chip > 0))
                def _():
                    hop(i, stages[i], chip, step, left, send_l, recv_l).wait_send()

            for origin in range(chips):
                hop(i, stages[i], origin, origin, partner, send_p, recv_p).wait()

    for copy in swap_copies:
        copy.wait()


def exchange(gathers, swaps, width, column, key):
    groups, shards = lax.axis_size("group"), lax.axis_size("shard")
    chips = shards // 2
    n_gather, n_swap = len(gathers), len(swaps)
    shapes, scratch = [], []
    for i, array in enumerate(gathers):
        block = array.shape[:-1] + (width if i == 0 else array.shape[-1],)
        shapes.append(jax.ShapeDtypeStruct((shards,) + block, array.dtype))
        scratch.append(pltpu.VMEM(block, array.dtype))
    for array in swaps:
        shapes.append(jax.ShapeDtypeStruct((groups - 1,) + array.shape[1:], array.dtype))
    dma = pltpu.SemaphoreType.DMA
    if n_gather:
        scratch += [dma((n_gather,)), dma((n_gather,))]
        scratch += [dma((n_gather, max(chips - 1, 1)))] * 4
        scratch += [dma((n_gather, chips))] * 2
    if n_swap:
        scratch += [dma((n_swap, groups - 1))] * 2
    return pl.pallas_call(
        functools.partial(exchange_kernel, n_gather, n_swap, width, column),
        out_shape=shapes,
        in_specs=[pl.BlockSpec(memory_space=pl.ANY)] * (n_gather + n_swap),
        out_specs=[pl.BlockSpec(memory_space=pl.ANY)] * (n_gather + n_swap),
        scratch_shapes=scratch,
        compiler_params=pltpu.CompilerParams(collective_id=key, has_side_effects=True),
    )(*gathers, *swaps)


def tally_kernel(per_step, iters, with_extra, owners, labels, extra, rows, sums, *more):
    step = pl.program_id(0)
    centers = sums.shape[2]
    block_rows = rows.shape[1]

    @pl.when(step == 0)
    def _():
        sums[...] = jnp.zeros_like(sums)
        if with_extra:
            more[0][...] = jnp.zeros_like(more[0])

    ids = lax.broadcasted_iota(jnp.int32, (centers, block_rows), 0)
    for block in range(per_step):
        owner = owners[step * per_step + block]
        for t in range(iters):
            onehot = (ids == labels[block, t : t + 1, :]).astype(jnp.bfloat16)
            sums[owner, t] += jnp.dot(
                onehot, rows[block], preferred_element_type=jnp.float32
            )
            if with_extra:
                more[0][owner, t] += lax.dot_general(
                    extra[block],
                    onehot,
                    (((1,), (1,)), ((), ())),
                    preferred_element_type=jnp.float32,
                )


def tally(owners, labels, extra, rows, groups, centers, per_step, with_extra):
    blocks, iters, block_rows = labels.shape
    width = rows.shape[-1]
    shapes = [jax.ShapeDtypeStruct((groups, iters, centers, width), jnp.float32)]
    if with_extra:
        shapes.append(jax.ShapeDtypeStruct((groups, iters, extra.shape[1], centers), jnp.float32))
    out_specs = [pl.BlockSpec(s.shape, lambda i, o: (0, 0, 0, 0)) for s in shapes]
    return pl.pallas_call(
        functools.partial(tally_kernel, per_step, iters, with_extra),
        out_shape=shapes,
        grid_spec=pltpu.PrefetchScalarGridSpec(
            num_scalar_prefetch=1,
            grid=(blocks // per_step,),
            in_specs=[
                pl.BlockSpec((per_step, iters, block_rows), lambda i, o: (i, 0, 0)),
                pl.BlockSpec((per_step,) + extra.shape[1:], lambda i, o: (i, 0, 0)),
                pl.BlockSpec((per_step, block_rows, width), lambda i, o: (i, 0, 0)),
            ],
            out_specs=out_specs,
        ),
        compiler_params=pltpu.CompilerParams(vmem_limit_bytes=48 * 2**20),
    )(owners, labels, extra, rows)


def body(embeddings, assignments, block_group, centroids):
    groups, shards = lax.axis_size("group"), lax.axis_size("shard")
    mine, place = lax.axis_index("group"), lax.axis_index("shard")
    local, block_rows, features = embeddings.shape
    iters = assignments.shape[1]
    owned = centroids.shape[1] // shards
    chunks = CHUNKS if features % (CHUNKS * 128) == 0 else 1
    width = features // chunks
    blocks = shards * local

    wide = embeddings.astype(jnp.float32)
    squares = jnp.sum(wide * wide, axis=2)
    meta = jnp.concatenate(
        [
            assignments.astype(jnp.float32),
            jnp.broadcast_to(
                block_group[:, None, None].astype(jnp.float32), (local, 1, block_rows)
            ),
            squares[:, None, :],
            jnp.zeros((local, META - iters - 2, block_rows), jnp.float32),
        ],
        axis=1,
    )

    rows, metas = exchange([embeddings, meta], [], width, 0, 0)
    metas = metas.reshape(blocks, META, block_rows)
    labels = metas[:, :iters].astype(jnp.int32) - place * owned
    owners = metas[:, iters, 0].astype(jnp.int32)
    square = metas[:, iters + 1]
    high = lax.reduce_precision(square, 8, 7)
    middle = lax.reduce_precision(square - high, 8, 7)
    low = square - high - middle
    one = jnp.ones_like(square)
    zero = jnp.zeros_like(square)
    extra = jnp.stack([one, high, middle, low] + [zero] * 12, axis=1).astype(jnp.bfloat16)

    totals = []
    tail = None
    pending = []
    for chunk in range(chunks):
        result = tally(
            owners,
            labels,
            extra,
            rows.reshape(blocks, block_rows, width),
            groups,
            owned,
            local,
            chunk == 0,
        )
        column = (chunk + 1) * width
        if chunk + 1 < chunks:
            rows, *got = exchange([embeddings], result, width, column, chunk + 1)
        else:
            got = exchange([], result, width, 0, chunk + 1)
        whole = [
            lax.dynamic_index_in_dim(kept, mine, 0, keepdims=False) + jnp.sum(came, axis=0)
            for kept, came in zip(result, got)
        ]
        totals.append(whole[0])
        if chunk == 0:
            tail = whole[1]

    prior = lax.dynamic_slice_in_dim(centroids[0], place * owned, owned, 0)
    counts = tail[:, 0]
    within = tail[iters - 1, 1] + tail[iters - 1, 2] + tail[iters - 1, 3]
    pieces = []
    for chunk in range(chunks):
        previous = prior[:, chunk * width : (chunk + 1) * width]
        for t in range(iters):
            sums = totals[chunk][t]
            count = counts[t][:, None]
            if t == iters - 1:
                within = within + jnp.sum(
                    previous * (count * previous - 2.0 * sums), axis=1
                )
            previous = (sums + PRIOR * previous) / (count + PRIOR)
        pieces.append(previous)
    inertia = within / ((counts[iters - 1] + PRIOR) * features)
    return (jnp.concatenate(pieces, axis=1)[None], inertia[None])


def solution(mesh):
    in_specs = (
        P(("group", "shard"), None, None),
        P(("group", "shard"), None, None),
        P(("group", "shard")),
        P("group", None, None),
    )
    out_specs = (P("group", "shard", None), P("group", "shard"))
    return jax.shard_map(body, mesh=mesh, in_specs=in_specs, out_specs=out_specs, check_vma=False)
```

time: 388 us -> 259 us (0.67)
  Pallas kernels: 0 us -> 224 us
  waiting for transfers between devices: 220 us -> 0 us
  matrix products: 84.7 us -> 0 us
  blocking collectives: 30.8 us -> 0 us
  between operations: 14.8 us -> 0.82 us
  starting transfers between devices: 9.61 us -> 0 us
  local copies, waits for them, and re-layouts: 4.53 us -> 8.46 us
    pallas_call x0 -> x7, Pallas kernels: none -> 224 us  [the longest x4 195 us: exchange(): pl.pallas_call(functools.partial(exchange_kernel, n_gather, n_swap, width...]
    reduce_scatter x2 -> x0, waiting for transfers between devices: 184 us -> none  [body(): reduced = lax.psum_scatter(totals, 'shard', scatter_dimension=0, tiled=True)]
    dot_general x14 -> x0, matrix products: 84.7 us -> none  [the longest x8 69.4 us: tally(): lax.dot_general(onehot.astype(jnp.bfloat16), piece_rows, (((0,), (0,)), (...]
    all_to_all x2 -> x0, waiting for transfers between devices: 35.6 us -> none  [the longest x1 35.6 us: body(): lax.all_to_all(sent_rows, 'group', split_axis=0, concat_axis=0, tiled=True)]
    unnamed x1 -> x0, blocking collectives: 30.8 us -> none
    all_to_all x2 -> x0, starting transfers between devices: 9.38 us -> none  [the longest x1 5.19 us: body(): lax.all_to_all(sent_labels, 'group', split_axis=0, concat_axis=0, tiled=T...]
    reduce_sum x14 -> x6, other arithmetic: 19.9 us -> 12.2 us  [the longest x4 9.64 us: body(): jnp.sum(came, axis=0)]
    unnamed x5 -> x10, local copies, waits for them, and re-layouts: 1.21 us -> 6.5 us
  transfers between devices with their start and end apart: 4 -> 0, of which waited for: 3 -> 0; matrix products, arithmetic and copies ran while one was open for 13% -> 0% of each run, Pallas kernels for 0% -> 0%
where the time goes in v1:
time: 259 us; the launch traced here: 258 us
  Pallas kernels  224 us (86%)
  other arithmetic  24.9 us (10%)
  local copies, waits for them, and re-layouts  8.46 us (3%)
    pallas_call x4, Pallas kernels, exchange(): pl.pallas_call(functools.partial(exchange_kernel, n_gather, n_swap, width...  195 us
    pallas_call x3, Pallas kernels, tally(): pl.pallas_call(functools.partial(tally_kernel, per_step, iters, with_extr...  29.4 us
    reduce_sum x4, other arithmetic, body(): jnp.sum(came, axis=0)  9.64 us
    unnamed x10, local copies, waits for them, and re-layouts  6.5 us

profile of v1, /device:TPU:0, one launch (start us, length us, event | category | flops | bytes accessed | tf_op | source)
XLA Modules:
  0.0 258.1 jit_solution(8858427478289250125)
XLA Ops:
  1.4 1.8 multiply_reduce_fusion
  3.2 0.7 convert_element_type.19
  4.6 1.5 dynamic-slice_bitcast_fusion
  6.1 44.9 %shard_map.59 = (bf16[8,4,256,256]{3,2,1,0:T(8,128)(2,1)}, f32[8,4,8,256]{3,2,1,0:T(8,128)}) custom-call(bf16[4,256,768]{2,1,0:T(8,128)(2,1)} %refs_0_.5, f32[4,8,256]{2,1,0:T(8,128)} %maximum_maximum_fusion.refs_1_), custom_call_target="tpu_custom_call" | custom-call | tf_op jit(solution)/shard_map/pallas_call | solution.py:178
  51.0 1.6 fusion.8.owners
  52.6 1.0 fusion.6.labels
  53.6 1.0 fusion.7
  55.0 11.9 %shard_map.60 = (f32[4,2,512,256]{3,2,1,0:T(8,128)S(1)}, f32[4,2,16,512]{3,2,1,0:T(8,128)S(1)}) custom-call(s32[32]{0:T(128)S(1)} %fusion.8.owners, s32[32,2,256]{2,1,0:T(2,128)S(1)} %fusion.6.labels, bf16[32,16,256]{2,1,0:T(8,128)(2,1)S(1)} %stack.15.extra, bf16[32,256,256]{2,1,0:T(8,128)(2,1)} %bitcast.73), custom_call_target="tpu_custom_call" | custom-call | tf_op jit(solution)/shard_map/pallas_call | solution.py:223
  66.9 1.9 copy-done.2
  69.5 52.4 %shard_map.61 = (bf16[8,4,256,256]{3,2,1,0:T(8,128)(2,1)}, f32[3,2,512,256]{3,2,1,0:T(8,128)}, f32[3,2,16,512]{3,2,1,0:T(8,128)}) custom-call(bf16[4,256,768]{2,1,0:T(8,128)(2,1)} %refs_0_.5, f32[4,2,512,256]{3,2,1,0:T(8,128)} %copy-done.2, f32[4,2,16,512]{3,2,1,0:T(8,128)} %copy-done.3), custom_call_target="tpu_custom_call" | custom-call | tf_op jit(solution)/shard_map/pallas_call | solution.py:178
  121.9 3.2 %reduce_sum.79 = f32[2,512,256]{2,1,0:T(8,128)} reduce(f32[3,2,512,256]{3,2,1,0:T(8,128)} %get-tuple-element.15, f32[]{:T(128)} %constant.14.clone.1), dimensions={0}, to_apply=%region_1.2 | reduce | flops 524288 | bytes 4194308 | tf_op jit(solution)/shard_map/reduce_sum | solution.py:296
  125.1 1.7 bitcast_add_fusion.2
  126.9 0.9 bitcast_add_fusion.3
  128.0 8.7 %shard_map.62.refs_1_ = f32[4,2,512,256]{3,2,1,0:T(8,128)S(1)} custom-call(s32[32]{0:T(128)S(1)} %fusion.8.owners, s32[32,2,256]{2,1,0:T(2,128)S(1)} %fusion.6.labels, bf16[32,16,256]{2,1,0:T(8,128)(2,1)S(1)} %stack.15.extra, bf16[32,256,256]{2,1,0:T(8,128)(2,1)} %bitcast.74), custom_call_target="tpu_custom_call" | custom-call | tf_op jit(solution)/shard_map/pallas_call | solution.py:223
  136.7 1.9 copy-done.1
  138.6 49.4 %shard_map.63 = (bf16[8,4,256,256]{3,2,1,0:T(8,128)(2,1)}, f32[3,2,512,256]{3,2,1,0:T(8,128)}) custom-call(bf16[4,256,768]{2,1,0:T(8,128)(2,1)} %refs_0_.5, f32[4,2,512,256]{3,2,1,0:T(8,128)} %copy-done.1), custom_call_target="tpu_custom_call" | custom-call | tf_op jit(solution)/shard_map/pallas_call | solution.py:178
  188.0 3.2 %reduce_sum.81 = f32[2,512,256]{2,1,0:T(8,128)} reduce(f32[3,2,512,256]{3,2,1,0:T(8,128)} %get-tuple-element.18, f32[]{:T(128)} %constant.14.clone.1), dimensions={0}, to_apply=%region_3.4 | reduce | flops 524288 | bytes 4194308 | tf_op jit(solution)/shard_map/reduce_sum | solution.py:296
  191.2 8.7 %shard_map.64.refs_0_ = f32[4,2,512,256]{3,2,1,0:T(8,128)S(1)} custom-call(s32[32]{0:T(128)S(1)} %fusion.8.owners, s32[32,2,256]{2,1,0:T(2,128)S(1)} %fusion.6.labels, bf16[32,16,256]{2,1,0:T(8,128)(2,1)S(1)} %stack.15.extra, bf16[32,256,256]{2,1,0:T(8,128)(2,1)} %bitcast.75), custom_call_target="tpu_custom_call" | custom-call | tf_op jit(solution)/shard_map/pallas_call | solution.py:223
  199.9 2.0 copy-done
  201.9 47.9 %shard_map.65 = f32[3,2,512,256]{3,2,1,0:T(8,128)} custom-call(f32[4,2,512,256]{3,2,1,0:T(8,128)} %copy-done), custom_call_target="tpu_custom_call" | custom-call | tf_op jit(solution)/shard_map/pallas_call | solution.py:178
  249.8 3.2 %reduce_sum.82 = f32[2,512,256]{2,1,0:T(8,128)} reduce(f32[3,2,512,256]{3,2,1,0:T(8,128)} %shard_map.65, f32[]{:T(128)} %constant.14.clone.1), dimensions={0}, to_apply=%region_4.5 | reduce | flops 524288 | bytes 4194308 | tf_op jit(solution)/shard_map/reduce_sum | solution.py:296
  253.0 2.4 bitcast_add_fusion
  255.5 0.8 multiply_reduce_fusion.3
  256.9 1.2 maximum_bitcast_fusion
  (22 shorter events, 3.3 us)
Async XLA Ops:
  66.9 1.9 copy-start.2
  68.8 0.7 copy-start.3
  121.9 4.9 %copy-start.4 = (f32[3,2,16,512]{3,2,1,0:T(8,128)S(1)}, f32[3,2,16,512]{3,2,1,0:T(8,128)}, u32[]{:S(2)}) copy-start(f32[3,2,16,512]{3,2,1,0:T(8,128)} %get-tuple-element.16) | copy-start | bytes 589828
  136.7 1.9 copy-start.1
  199.9 2.0 copy-start
